TPU v7x, 32 devices: a whole 2x2x4 slice. The times are simulated.
32 devices in a mesh: expert: 4 (over z), neuron: 8 (over y, x, core).
Axes of the slice: x: 2, y: 2, z: 4, core: 2. Of those that a mesh axis runs over, the one named last changes fastest.
Arguments:
- tokens: bfloat16 [256, 4096], P('neuron'), may hold values from -6 to 6
- route_logits: float32 [256, 2], replicated, may hold values from -6 to 6
- expert_ids: int32 [256, 2], replicated, may hold values from 0 to 3, all different within a row; in each aligned block of 256 rows (0 to 255, 256 to 511, ...) at most 128 rows name the same one
- block_live: int32 [4, 224], P('expert', 'neuron'), may hold values 0 or 1
- w_gate: bfloat16 [4, 4096, 14336], P('expert', None, 'neuron'), may hold values from -0.09375 to 0.09375
- w_up: bfloat16 [4, 4096, 14336], P('expert', None, 'neuron'), may hold values from -0.09375 to 0.09375
- w_down: bfloat16 [4, 14336, 4096], P('expert', 'neuron'), may hold values from -0.046875 to 0.046875
Outputs:
- mixed: bfloat16 [256, 4096], P('neuron')
Inputs may be any that keep to these rules, and one draw needn't show every extreme that they name: `expert_ids`: each token names two different experts; no expert is named by more than 128 tokens, a bound that some block reaches; every expert is named.
All inputs are finite; a program needn't handle non-finite values. No bound on the sum of `block_live` on one device may be relied on, other than what follows from the above.
Results may differ from a plain program's by a relative error of at most 0.0049.
Values may be sent and summed in bfloat16 or wider, within the bound.
A program may use at most 128 MiB of HBM per device.

v0:
```python
import jax
import jax.numpy as jnp
from jax import lax
from jax.sharding import PartitionSpec as P

BLK = 64


def routing(expert_ids, route_logits, expert, capacity):
    chosen = (expert_ids == expert).astype(jnp.int32)
    flat_hits = chosen.reshape(-1)
    before = (jnp.cumsum(flat_hits) - flat_hits).reshape(chosen.shape)
    slot_pair = jnp.where(chosen > 0, before, capacity)
    leading = jax.nn.sigmoid(route_logits[:, 0] - route_logits[:, 1])
    mix_gates = jnp.stack([leading, 1.0 - leading], axis=1)
    weight = jnp.sum(mix_gates * chosen.astype(jnp.float32), axis=1)
    slot_tok = jnp.min(slot_pair, axis=1)
    slot_index = lax.broadcasted_iota(jnp.int32, (capacity, expert_ids.shape[0]), 0)
    dispatch = (
        (slot_pair[None, :, 0] == slot_index) | (slot_pair[None, :, 1] == slot_index)
    ).astype(jnp.bfloat16)
    return (dispatch, slot_tok, weight)


def per_device(tokens, route_logits, expert_ids, block_live, w_gate, w_up, w_down):
    total_tokens = expert_ids.shape[0]
    capacity = total_tokens // 2
    expert = lax.axis_index("expert")
    dispatch, slot_tok, weight = routing(expert_ids, route_logits, expert, capacity)
    gathered = jnp.dot(
        dispatch,
        lax.all_gather(tokens, "neuron", axis=0, tiled=True),
        preferred_element_type=jnp.float32,
    ).astype(jnp.bfloat16)
    gate_val = jnp.dot(gathered, w_gate[0], preferred_element_type=jnp.float32)
    up_val = jnp.dot(gathered, w_up[0], preferred_element_type=jnp.float32)
    live = jnp.repeat(block_live[0].astype(jnp.float32), BLK)
    hidden = (jax.nn.silu(gate_val) * up_val * live[None, :]).astype(jnp.bfloat16)
    partial_value = jnp.dot(hidden, w_down[0], preferred_element_type=jnp.float32)
    picked = jnp.take(partial_value, jnp.minimum(slot_tok, capacity - 1), axis=0)
    weighted = weight[:, None] * picked
    own_part = lax.psum_scatter(weighted, "neuron", scatter_dimension=0, tiled=True)
    mixed = lax.psum(own_part, "expert")
    return mixed.astype(jnp.bfloat16)


def solution(mesh):
    placed = (
        P("neuron", None),
        P(),
        P(),
        P("expert", "neuron"),
        P("expert", None, "neuron"),
        P("expert", None, "neuron"),
        P("expert", "neuron", None),
    )
    return jax.shard_map(
        per_device, mesh=mesh, in_specs=placed, out_specs=P("neuron", None), check_vma=False
    )
```

profile of v0, /device:TPU:0, one launch (start us, length us, event | category | flops | bytes accessed | tf_op | source)
XLA Modules:
  0.0 162.3 jit_solution(13914430239259568634)
XLA Ops:
  6.5 0.0 all-gather.2.cloned.1.call-start
  6.5 0.7 all-gather.2.cloned.1.call-update
  7.3 0.0 reduce-scatter.2.cloned.1.call-start
  7.3 0.8 broadcast_subtract_fusion
  8.1 0.7 fusion.23
  8.8 0.1 copy.21
  8.9 0.1 reshape.51
  9.1 0.3 reduce-window.9
  9.4 0.1 slice.21
  9.5 0.1 reshape.52
  9.6 0.7 convert_bitcast_fusion
  10.3 0.1 broadcast_in_dim.20
  10.3 0.1 mul.32
  10.4 0.1 slice_reduce_fusion
  10.6 0.1 broadcast.55
  10.6 0.1 reshape.54
  10.7 0.1 copy.22
  10.9 28.9 %all-gather.2.cloned.1.call-done = bf16[256,4096]{1,0:T(8,128)(2,1)} async-done(((bf16[32,4096]{1,0:T(8,128)(2,1)}), bf16[256,4096]{1,0:T(8,128)(2,1)}) %all-gather.2.cloned.1.call-update) | async-done | bytes 2097168 | tf_op jit(solution)/shard_map/all_gather | solution.py:32
  39.8 2.0 %convolution_convert_fusion = bf16[128,4096]{1,0:T(8,128)(2,1)S(1)} fusion(bf16[256,4096]{1,0:T(8,128)(2,1)} %all-gather.2.cloned.1.call-done, s32[256]{0:T(256)S(1)} %bitcast.27, s32[256]{0:T(256)S(1)} %bitcast.26), kind=kOutput, calls=%fused_computation.7 | convolution fusion | flops 269058048 | bytes 3147776 | tf_op jit(solution)/shard_map/dot_general | solution.py:30
  41.8 8.2 %fusion.4 = f32[128,1792]{1,0:T(8,128)} fusion(bf16[128,4096]{1,0:T(8,128)(2,1)S(1)} %convolution_convert_fusion, bf16[1,4096,1792]{2,1,0:T(8,128)(2,1)} %param.11), kind=kOutput, calls=%fused_computation.5 | convolution fusion | flops 1879048192 | bytes 16646144 | tf_op jit(solution)/shard_map/dot_general | solution.py:35
  50.0 14.1 %fusion = f32[128,4096]{1,0:T(8,128)S(1)} fusion(bf16[1,1792,4096]{2,1,0:T(8,128)(2,1)} %param.13, bf16[128,4096]{1,0:T(8,128)(2,1)S(1)} %convolution_convert_fusion, bf16[1,4096,1792]{2,1,0:T(8,128)(2,1)} %param.12, f32[128,1792]{1,0:T(8,128)} %fusion.4, f32[1792]{0:T(1024)S(1)} %mul.32), kind=kOutput, calls=%fused_computation.1 | convolution fusion | flops 3759702016 | bytes 33430528 | tf_op jit(solution)/shard_map/dot_general | solution.py:39
  64.1 3.8 %gather_fusion = f32[256,4096]{1,0:T(8,128)} fusion(f32[128,4096]{1,0:T(8,128)S(1)} %fusion, s32[1024]{0:T(1024)S(1)} %pad_clamp_fusion), kind=kCustom, calls=%fused_computation | custom fusion | bytes 8389632 | tf_op jit(solution)/shard_map/jit(_take)/gather | solution.py:40
  67.9 4.9 %select_multiply_fusion = f32[256,4096]{1,0:T(8,128)} fusion(f32[256,4096]{1,0:T(8,128)} %gather_fusion, f32[256]{0:T(256)S(1)} %get-tuple-element.5, pred[256]{0:T(512)(128)(4,1)S(1)} %compare_and_fusion), kind=kLoop, calls=%fused_computation.8 | loop fusion | flops 2097152 | bytes 8389888 | tf_op jit(solution)/shard_map/mul | solution.py:41
  72.8 0.0 reduce-scatter.2.cloned.1.call-update
  72.8 51.3 %reduce-scatter.2.cloned.1.call-done = f32[32,4096]{1,0:T(8,128)} async-done(((f32[256,4096]{1,0:T(8,128)}), f32[32,4096]{1,0:T(8,128)}) %reduce-scatter.2.cloned.1.call-update) | async-done | bytes 524304 | tf_op jit(solution)/shard_map/reduce_scatter | solution.py:42
  124.1 31.4 %all-reduce.1 = bf16[32,4096]{1,0:T(8,128)(2,1)} all-reduce(f32[32,4096]{1,0:T(8,128)} %reduce-scatter.2.cloned.1.call-done), channel_id=1, replica_groups=mesh['expert'=4,'neuron'=8] {'expert'}, use_global_device_ids=true, to_apply=%region_5.6 | all-reduce | flops 131072 | bytes 786432 | tf_op jit(solution)/shard_map/psum | solution.py:43
  (7 shorter events, 0.1 us)
Async XLA Ops:
  6.5 33.2 %all-gather.2.cloned.1.call-start = ((), (), s32[]{:S(2)}) async-start(), calls=%async_computation.1 | async-start | bytes 2359296 | tf_op jit(solution)/shard_map/all_gather | solution.py:32
  7.3 116.8 %reduce-scatter.2.cloned.1.call-start = ((), (), s32[]{:S(2)}) async-start(), calls=%async_computation.2 | async-start | bytes 4718592 | tf_op jit(solution)/shard_map/reduce_scatter | solution.py:42
Sparse Core Ops, SparseCore 0:
  9.2 30.5 all-gather.1
  72.9 51.1 reduce-scatter.1
where the time goes:
time: 163 us; the launch traced here: 162 us
  waiting for transfers between devices  80.9 us (50%)
  blocking collectives  31.4 us (19%)
  matrix products  24.3 us (15%)
  between operations  13.5 us (8%)
  other arithmetic  7.42 us (5%)
  local copies, waits for them, and re-layouts  4.83 us (3%)
    reduce_scatter x1, waiting for transfers between devices, per_device(): lax.psum_scatter(weighted, 'neuron', scatter_dimension=0, tiled=True)  51.3 us
    psum x1, blocking collectives, per_device(): mixed = lax.psum(own_part, 'expert')  31.4 us
    all_gather x1, waiting for transfers between devices, per_device(): lax.all_gather(tokens, 'neuron', axis=0, tiled=True)  28.9 us
    dot_general x1, matrix products, per_device(): jnp.dot(hidden, w_down[0], preferred_element_type=jnp.float32)  14.1 us
    dot_general x1, matrix products, per_device(): gate_val = jnp.dot(gathered, w_gate[0], preferred_element_type=jnp.float32)  8.18 us
    mul x1, other arithmetic, per_device(): weighted = weight[:, None] * picked  4.89 us
    gather x1, local copies, waits for them, and re-layouts, per_device(): jnp.take(partial_value, jnp.minimum(slot_tok, capacity - 1), axis=0)  3.82 us
  transfers between devices with their start and end apart: 2, of which 2 were waited for; matrix products, arithmetic and copies ran while one was open for 2% of the time, Pallas kernels for 0%

commit v1 on v0

--- a/solution.py
+++ b/solution.py
@@ -40,7 +40,7 @@
     picked = jnp.take(partial_value, jnp.minimum(slot_tok, capacity - 1), axis=0)
     weighted = weight[:, None] * picked
     own_part = lax.psum_scatter(weighted, "neuron", scatter_dimension=0, tiled=True)
-    mixed = lax.psum(own_part, "expert")
+    mixed = jnp.sum(lax.all_gather(own_part, "expert"), axis=0)
     return mixed.astype(jnp.bfloat16)
 
 

time: 163 us -> 181 us (1.11)
  waiting for transfers between devices: 80.9 us -> 128 us
  blocking collectives: 31.4 us -> 0 us
  other arithmetic: 7.42 us -> 9.9 us
    all_gather x0 -> x1, waiting for transfers between devices: none -> 47.2 us  [per_device(): mixed = jnp.sum(lax.all_gather(own_part, 'expert'), axis=0)]
    psum x1 -> x0, blocking collectives: 31.4 us -> none  [per_device(): mixed = lax.psum(own_part, 'expert')]
    reduce_sum x0 -> x1, other arithmetic: none -> 2.48 us  [per_device(): mixed = jnp.sum(lax.all_gather(own_part, 'expert'), axis=0)]
  transfers between devices with their start and end apart: 2 -> 3, of which waited for: 2 -> 3; matrix products, arithmetic and copies ran while one was open for 2% -> 2% of each run, Pallas kernels for 0% -> 0%
where the time goes in v1:
time: 181 us; the launch traced here: 180 us
  waiting for transfers between devices  128 us (71%)
  matrix products  24.3 us (13%)
  between operations  13.2 us (7%)
  other arithmetic  9.9 us (5%)
  local copies, waits for them, and re-layouts  4.83 us (3%)
    reduce_scatter x1, waiting for transfers between devices, per_device(): lax.psum_scatter(weighted, 'neuron', scatter_dimension=0, tiled=True)  51.2 us
    all_gather x1, waiting for transfers between devices, per_device(): mixed = jnp.sum(lax.all_gather(own_part, 'expert'), axis=0)  47.2 us
    all_gather x1, waiting for transfers between devices, per_device(): lax.all_gather(tokens, 'neuron', axis=0, tiled=True)  28.9 us
    dot_general x1, matrix products, per_device(): jnp.dot(hidden, w_down[0], preferred_element_type=jnp.float32)  14.1 us
    dot_general x1, matrix products, per_device(): gate_val = jnp.dot(gathered, w_gate[0], preferred_element_type=jnp.float32)  8.18 us
    mul x1, other arithmetic, per_device(): weighted = weight[:, None] * picked  4.89 us
    gather x1, local copies, waits for them, and re-layouts, per_device(): jnp.take(partial_value, jnp.minimum(slot_tok, capacity - 1), axis=0)  3.82 us
  transfers between devices with their start and end apart: 3, of which 3 were waited for; matrix products, arithmetic and copies ran while one was open for 2% of the time, Pallas kernels for 0%

profile of v1, /device:TPU:0, one launch (start us, length us, event | category | flops | bytes accessed | tf_op | source)
XLA Modules:
  0.0 180.4 jit_solution(16449406159779286116)
XLA Ops:
  6.5 0.0 all-gather.4.cloned.1.call-start
  6.5 0.7 all-gather.4.cloned.1.call-update
  7.3 0.0 reduce-scatter.2.cloned.1.call-start
  7.3 0.8 broadcast_subtract_fusion
  8.1 0.7 fusion.23
  8.8 0.1 copy.21
  8.9 0.1 reshape.51
  9.1 0.3 reduce-window.9
  9.4 0.1 slice.21
  9.5 0.1 reshape.52
  9.6 0.7 convert_bitcast_fusion
  10.3 0.1 broadcast_in_dim.20
  10.3 0.1 mul.32
  10.4 0.1 slice_reduce_fusion
  10.6 0.1 broadcast.55
  10.6 0.1 reshape.54
  10.7 0.1 copy.22
  10.9 28.9 %all-gather.4.cloned.1.call-done = bf16[256,4096]{1,0:T(8,128)(2,1)} async-done(((bf16[32,4096]{1,0:T(8,128)(2,1)}), bf16[256,4096]{1,0:T(8,128)(2,1)}) %all-gather.4.cloned.1.call-update) | async-done | bytes 2097168 | tf_op jit(solution)/shard_map/all_gather | solution.py:32
  39.8 2.0 %convolution_convert_fusion = bf16[128,4096]{1,0:T(8,128)(2,1)S(1)} fusion(bf16[256,4096]{1,0:T(8,128)(2,1)} %all-gather.4.cloned.1.call-done, s32[256]{0:T(256)S(1)} %bitcast.29, s32[256]{0:T(256)S(1)} %bitcast.28), kind=kOutput, calls=%fused_computation.7 | convolution fusion | flops 269058048 | bytes 3147776 | tf_op jit(solution)/shard_map/dot_general | solution.py:30
  41.8 8.2 %fusion.4 = f32[128,1792]{1,0:T(8,128)} fusion(bf16[128,4096]{1,0:T(8,128)(2,1)S(1)} %convolution_convert_fusion, bf16[1,4096,1792]{2,1,0:T(8,128)(2,1)} %param.11), kind=kOutput, calls=%fused_computation.5 | convolution fusion | flops 1879048192 | bytes 16646144 | tf_op jit(solution)/shard_map/dot_general | solution.py:35
  50.0 14.1 %fusion = f32[128,4096]{1,0:T(8,128)S(1)} fusion(bf16[1,1792,4096]{2,1,0:T(8,128)(2,1)} %param.13, bf16[128,4096]{1,0:T(8,128)(2,1)S(1)} %convolution_convert_fusion, bf16[1,4096,1792]{2,1,0:T(8,128)(2,1)} %param.12, f32[128,1792]{1,0:T(8,128)} %fusion.4, f32[1792]{0:T(1024)S(1)} %mul.32), kind=kOutput, calls=%fused_computation.1 | convolution fusion | flops 3759702016 | bytes 33430528 | tf_op jit(solution)/shard_map/dot_general | solution.py:39
  64.1 3.8 %gather_fusion = f32[256,4096]{1,0:T(8,128)} fusion(f32[128,4096]{1,0:T(8,128)S(1)} %fusion, s32[1024]{0:T(1024)S(1)} %pad_clamp_fusion), kind=kCustom, calls=%fused_computation | custom fusion | bytes 8389632 | tf_op jit(solution)/shard_map/jit(_take)/gather | solution.py:40
  67.9 4.9 %select_multiply_fusion = f32[256,4096]{1,0:T(8,128)} fusion(f32[256,4096]{1,0:T(8,128)} %gather_fusion, f32[256]{0:T(256)S(1)} %get-tuple-element.5, pred[256]{0:T(512)(128)(4,1)S(1)} %compare_and_fusion), kind=kLoop, calls=%fused_computation.8 | loop fusion | flops 2097152 | bytes 8389888 | tf_op jit(solution)/shard_map/mul | solution.py:41
  72.8 0.0 reduce-scatter.2.cloned.1.call-update
  72.8 0.0 all-gather.6.cloned.1.call-start
  72.9 51.2 %reduce-scatter.2.cloned.1.call-done = f32[32,4096]{1,0:T(8,128)} async-done(((f32[256,4096]{1,0:T(8,128)}), f32[32,4096]{1,0:T(8,128)}) %reduce-scatter.2.cloned.1.call-update) | async-done | bytes 524304 | tf_op jit(solution)/shard_map/reduce_scatter | solution.py:42
  124.1 0.0 all-gather.6.cloned.1.call-update
  124.1 47.2 %all-gather.6.cloned.1.call-done = f32[128,4096]{1,0:T(8,128)} async-done(((f32[32,4096]{1,0:T(8,128)}), f32[128,4096]{1,0:T(8,128)}) %all-gather.6.cloned.1.call-update) | async-done | bytes 2097168 | tf_op jit(solution)/shard_map/all_gather | solution.py:43
  171.4 2.5 %reduce_sum.19 = bf16[32,4096]{1,0:T(8,128)(2,1)} reduce(f32[4,32,4096]{2,1,0:T(8,128)} %bitcast.27, f32[]{:T(128)} %constant.15.clone.1), dimensions={0}, to_apply=%region_5.6 | reduce | flops 393216 | bytes 2359300 | tf_op jit(solution)/shard_map/reduce_sum | solution.py:43
  (7 shorter events, 0.1 us)
Async XLA Ops:
  6.5 33.2 %all-gather.4.cloned.1.call-start = ((), (), s32[]{:S(2)}) async-start(), calls=%async_computation.1 | async-start | bytes 2359296 | tf_op jit(solution)/shard_map/all_gather | solution.py:32
  7.3 116.8 %reduce-scatter.2.cloned.1.call-start = ((), (), s32[]{:S(2)}) async-start(), calls=%async_computation.2 | async-start | bytes 4718592 | tf_op jit(solution)/shard_map/reduce_scatter | solution.py:42
  72.8 98.5 %all-gather.6.cloned.1.call-start = ((), (), s32[]{:S(2)}) async-start(), calls=%async_computation.3 | async-start | bytes 2621440 | tf_op jit(solution)/shard_map/all_gather | solution.py:43
Sparse Core Ops, SparseCore 0:
  9.2 30.5 all-gather.3
  72.9 51.1 reduce-scatter.1
  125.7 45.6 all-gather.5
